TPU v7x, 32 devices: a whole 2x2x4 slice. The times are simulated.
32 devices in a mesh: row: 16 (over z, y, core), col: 2 (over x).
Axes of the slice: x: 2, y: 2, z: 4, core: 2. Of those that a mesh axis runs over, the one named last changes fastest.
Arguments:
- pair: bfloat16 [256, 256, 128], P('row', 'col'), may hold values from -6 to 6
- relpos: bfloat16 [128, 128], replicated, may hold values from -4 to 4
- pair_gain: float32 [128], replicated, may hold values from 0.1 to 1.9
- bias_weight: bfloat16 [128, 12], replicated, may hold values from -0.5 to 0.5
- single: float32 [256, 384], P(('row', 'col')), may hold values from -6 to 6
- rotation_params: float32 [3, 256], P(None, ('row', 'col')), may hold values from -4 to 4
- translation: float32 [3, 256], P(None, ('row', 'col')), may hold values from -9 to 9
- residue_index: int32 [256], P(('row', 'col')), may hold values from 0 to 50944, as said below
- residue_mask: int32 [256], P(('row', 'col')), may hold values 0 or 1
- w_scalar: float32 [384, 576], replicated, may hold values from -0.3125 to 0.3125
- w_points: float32 [384, 576], replicated, may hold values from -0.3125 to 0.3125
- head_weights: float32 [12], replicated, may hold values from -2 to 1.5
- w_out: float32 [2112, 384], replicated, may hold values from -0.125 to 0.125
- w_hidden: float32 [384, 384], replicated, may hold values from -0.3125 to 0.3125
- w_back: float32 [384, 384], replicated, may hold values from -0.3125 to 0.3125
- w_frame: float32 [384, 6], replicated, may hold values from -0.078125 to 0.078125
Outputs:
- single_out: float32 [256, 384], P(('row', 'col'))
- frames: float32 [12, 256], P(None, ('row', 'col'))
Inputs may be any that keep to these rules, and one draw needn't show every extreme that they name: residue_index is strictly increasing along the crop, begins at 0 and ends at exactly 50944.
All inputs are finite; a program needn't handle non-finite values. No bound on the sum of `residue_mask` on one device may be relied on, other than what follows from the above.
Results may differ from a plain program's by a relative error of at most 0.0025.
Values may be sent and summed in bfloat16 or wider, within the bound.
A program may use at most 64 MiB of HBM per device.

v0:
```python
import math
import jax
import jax.numpy as jnp
from jax import lax
from jax.sharding import PartitionSpec as P

H = 12
C = 16
PQ = 4
PV = 8
BINS = 128
ITERS = 3
NORM_EPSILON = 1e-05
MASKED_LOGIT = -100000.0
NORM_FLOOR = 0.1
HIGHEST_PRECISION = lax.Precision.HIGHEST


def broadcast(value, axis, root):
    mine = lax.axis_index(axis) == root
    return lax.psum(jnp.where(mine, value, jnp.zeros_like(value)), axis)


def joined(part, axis, combine):
    gathered = jax.tree.map(lambda a: lax.all_gather(a, axis), part)

    def take(source):
        return jax.tree.map(lambda a: lax.dynamic_index_in_dim(a, source, 0, False), gathered)

    return lax.fori_loop(
        1, lax.axis_size(axis), lambda source, state: combine(state, take(source)), take(0)
    )


def layer_norm(values):
    center = values - jnp.mean(values, axis=-1, keepdims=True)
    spread = jnp.mean(center * center, axis=-1, keepdims=True)
    return center * lax.rsqrt(spread + NORM_EPSILON)


def rotation_from(update):
    quat_b, quat_c, quat_d = (update[0], update[1], update[2])
    inverse = 1.0 / (1.0 + quat_b * quat_b + quat_c * quat_c + quat_d * quat_d)
    entries = [
        1.0 + quat_b * quat_b - quat_c * quat_c - quat_d * quat_d,
        2.0 * (quat_b * quat_c - quat_d),
        2.0 * (quat_b * quat_d + quat_c),
        2.0 * (quat_b * quat_c + quat_d),
        1.0 - quat_b * quat_b + quat_c * quat_c - quat_d * quat_d,
        2.0 * (quat_c * quat_d - quat_b),
        2.0 * (quat_b * quat_d - quat_c),
        2.0 * (quat_c * quat_d + quat_b),
        1.0 - quat_b * quat_b - quat_c * quat_c + quat_d * quat_d,
    ]
    return jnp.stack(entries) * inverse


def to_global(rotation, points, translation):
    return jnp.stack(
        [
            rotation[3 * component] * points[0]
            + rotation[3 * component + 1] * points[1]
            + rotation[3 * component + 2] * points[2]
            + translation[component]
            for component in range(3)
        ]
    )


def to_local(rotation, points, translation):
    moved = [points[component] - translation[component] for component in range(3)]
    return jnp.stack(
        [
            rotation[component] * moved[0]
            + rotation[3 + component] * moved[1]
            + rotation[6 + component] * moved[2]
            for component in range(3)
        ]
    )


def compose(rotation, translation, update):
    turn = rotation_from(update[:3])
    new_rotation = jnp.stack(
        [
            rotation[3 * left] * turn[right]
            + rotation[3 * left + 1] * turn[3 + right]
            + rotation[3 * left + 2] * turn[6 + right]
            for left in range(3)
            for right in range(3)
        ]
    )
    new_translation = jnp.stack(
        [
            rotation[3 * left] * update[3]
            + rotation[3 * left + 1] * update[4]
            + rotation[3 * left + 2] * update[5]
            + translation[left]
            for left in range(3)
        ]
    )
    return (new_rotation, new_translation)


def project(single, rotation, translation, w_scalar, w_points):
    count = single.shape[0]
    scalars = jnp.dot(
        single, w_scalar, precision=HIGHEST_PRECISION, preferred_element_type=jnp.float32
    ).T
    scalars = scalars.reshape(3, H * C, count).astype(jnp.bfloat16)
    points = jnp.dot(
        single, w_points, precision=HIGHEST_PRECISION, preferred_element_type=jnp.float32
    ).T
    query_local = points[: 3 * H * PQ].reshape(3, H * PQ, count)
    key_local = points[3 * H * PQ : 6 * H * PQ].reshape(3, H * PQ, count)
    value_local = points[6 * H * PQ :].reshape(3, H * PV, count)
    return (
        scalars,
        to_global(rotation, query_local, translation),
        to_global(rotation, key_local, translation),
        to_global(rotation, value_local, translation),
    )


def advance(
    single, rotation, translation, scalar_out, point_out, pair_out, w_out, w_hidden, w_back, w_frame
):
    count = single.shape[0]
    local = to_local(rotation, point_out, translation)
    lengths = jnp.sqrt(jnp.sum(local * local, axis=0) + NORM_FLOOR)
    features = jnp.concatenate(
        [scalar_out, local.reshape(3 * H * PV, count), lengths, pair_out], axis=0
    )
    mixed = jnp.dot(
        features.T, w_out, precision=HIGHEST_PRECISION, preferred_element_type=jnp.float32
    )
    single = layer_norm(single + mixed)
    hidden = jax.nn.relu(
        jnp.dot(single, w_hidden, precision=HIGHEST_PRECISION, preferred_element_type=jnp.float32)
    )
    single = layer_norm(
        single
        + jnp.dot(hidden, w_back, precision=HIGHEST_PRECISION, preferred_element_type=jnp.float32)
    )
    update = jnp.dot(
        single, w_frame, precision=HIGHEST_PRECISION, preferred_element_type=jnp.float32
    ).T
    rotation, translation = compose(rotation, translation, update)
    return (single, rotation, translation)


def attend_block(
    query, keyval, query_side, key_side, value_side, bias, normed, pair_live, point_scale
):
    heads_query = query.reshape(H, C, -1)
    keys = keyval[0].reshape(H, C, -1)
    values = keyval[1].reshape(H, C, -1)
    query_grid = query_side.reshape(3, H, PQ, -1)
    key_grid = key_side.reshape(3, H, PQ, -1)
    value_grid = value_side.reshape(3, H, PV, -1)
    scores = jnp.einsum(
        "hci,hcj->hij", heads_query, keys, preferred_element_type=jnp.float32
    ) / math.sqrt(C)
    cross = jnp.einsum("ahpi,ahpj->hij", query_grid, key_grid, precision=HIGHEST_PRECISION)
    distance = (
        jnp.sum(query_grid * query_grid, axis=(0, 2))[:, :, None]
        + jnp.sum(key_grid * key_grid, axis=(0, 2))[:, None, :]
        - 2.0 * cross
    )
    logits = math.sqrt(1.0 / 3.0) * (scores + bias - point_scale[:, None, None] * distance)
    logits = jnp.where(pair_live[None], logits, MASKED_LOGIT)
    local_max = jnp.max(logits, axis=-1)
    unscaled = jnp.exp(logits - local_max[:, :, None])
    total_weight = jnp.sum(unscaled, axis=-1)
    rounded = unscaled.astype(jnp.bfloat16)
    scalar_sum = jnp.einsum("hij,hcj->hci", rounded, values, preferred_element_type=jnp.float32)
    point_sum = jnp.einsum("hij,ahpj->ahpi", unscaled, value_grid, precision=HIGHEST_PRECISION)
    pair_sum = jnp.einsum("hij,ijc->hci", rounded, normed, preferred_element_type=jnp.float32)
    return (local_max, total_weight, scalar_sum, point_sum, pair_sum)


def merge_softmax(first, second):
    top = jnp.maximum(first[0], second[0])
    lead = jnp.exp(first[0] - top)
    trail = jnp.exp(second[0] - top)
    return (
        top,
        first[1] * lead + second[1] * trail,
        first[2] * lead[:, None, :] + second[2] * trail[:, None, :],
        first[3] * lead[None, :, None, :] + second[3] * trail[None, :, None, :],
        first[4] * lead[:, None, :] + second[4] * trail[:, None, :],
    )


def body(
    pair,
    relpos,
    pair_gain,
    bias_weight,
    single,
    rotation_params,
    translation,
    residue_index,
    residue_mask,
    w_scalar,
    w_points,
    head_weights,
    w_out,
    w_hidden,
    w_back,
    w_frame,
):
    row_rows = pair.shape[0]
    col_rows = pair.shape[1]
    owned = single.shape[0]
    row_place = lax.axis_index("row")
    col_place = lax.axis_index("col")
    index_all, mask_all = (
        lax.all_gather(residue_index, ("row", "col"), axis=0, tiled=True),
        lax.all_gather(residue_mask, ("row", "col"), axis=0, tiled=True),
    )
    query_index = lax.dynamic_slice_in_dim(index_all, row_place * row_rows, row_rows, 0)
    key_index = lax.dynamic_slice_in_dim(index_all, col_place * col_rows, col_rows, 0)
    query_live = lax.dynamic_slice_in_dim(mask_all, row_place * row_rows, row_rows, 0) == 1
    key_live = lax.dynamic_slice_in_dim(mask_all, col_place * col_rows, col_rows, 0) == 1
    pair_live = query_live[:, None] & key_live[None, :]
    span_rows = math.gcd(row_rows, 64)

    def prepare(index):
        offset = (
            jnp.clip(key_index[None, :] - query_index[:, None], -(BINS // 2), BINS // 2 - 1)
            + BINS // 2
        )
        onehot = (offset[:, :, None] == lax.broadcasted_iota(jnp.int32, (1, 1, BINS), 2)).astype(
            jnp.bfloat16
        )
        embedded = jnp.dot(
            onehot.reshape(span_rows * col_rows, BINS), relpos, preferred_element_type=jnp.float32
        )
        summed = pair.astype(jnp.float32) + embedded.reshape(span_rows, col_rows, -1)
        normed_part = (layer_norm(summed) * pair_gain).astype(jnp.bfloat16)
        bias_part = jnp.einsum(
            "ijc,ch->hij", normed_part, bias_weight, preferred_element_type=jnp.float32
        )
        return (normed_part, bias_part)

    normed_blocks, bias_blocks = lax.map(
        prepare, jnp.arange(row_rows // span_rows, dtype=jnp.int32)
    )
    normed = normed_blocks.reshape(row_rows, col_rows, -1)
    bias = bias_blocks.transpose(1, 0, 2, 3).reshape(H, row_rows, col_rows)
    point_scale = jax.nn.softplus(head_weights) * (math.sqrt(2.0 / (9.0 * PQ)) / 2.0)
    rotation = rotation_from(rotation_params)
    state = single
    for step in range(ITERS):
        scalars, query_points, key_points, value_points = project(
            state, rotation, translation, w_scalar, w_points
        )
        query_flat = query_points.reshape(-1, owned)
        key_flat = key_points.reshape(-1, owned)
        value_flat = value_points.reshape(-1, owned)
        block_scalar = lax.all_gather(scalars, "col", axis=2, tiled=True)
        block_point = (
            lax.all_gather(query_flat, "col", axis=1, tiled=True),
            lax.all_gather(key_flat, "col", axis=1, tiled=True),
            lax.all_gather(value_flat, "col", axis=1, tiled=True),
        )
        query = block_scalar[0]
        query_side = block_point[0]
        ratio = lax.axis_size("row") // lax.axis_size("col")
        scalar_pieces = []
        key_pieces = []
        value_pieces = []
        for part in range(ratio):
            root = col_place * ratio + part
            scalar_pieces.append(broadcast(block_scalar[1:], "row", root))
            key_piece, value_piece = (
                broadcast(block_point[1], "row", root),
                broadcast(block_point[2], "row", root),
            )
            key_pieces.append(key_piece)
            value_pieces.append(value_piece)
        keyval = jnp.concatenate(scalar_pieces, axis=2)
        key_side = jnp.concatenate(key_pieces, axis=1)
        value_side = jnp.concatenate(value_pieces, axis=1)
        local_max, total_weight, scalar_sum, point_sum, pair_sum = attend_block(
            query, keyval, query_side, key_side, value_side, bias, normed, pair_live, point_scale
        )
        pair_out = None
        merged = joined(
            (local_max, total_weight, scalar_sum, point_sum, pair_sum), "col", merge_softmax
        )
        begin = col_place * owned
        total = lax.dynamic_slice_in_dim(merged[1], begin, owned, 1)
        scalar_share = lax.dynamic_slice_in_dim(merged[2], begin, owned, 2)
        point_share = lax.dynamic_slice_in_dim(merged[3], begin, owned, 3)
        pair_share = lax.dynamic_slice_in_dim(merged[4], begin, owned, 2)
        scalar_out = (scalar_share / total[:, None, :]).reshape(H * C, owned)
        point_out = (point_share / total[None, :, None, :]).reshape(3, H * PV, owned)
        pair_out = (pair_share / total[:, None, :]).reshape(-1, owned)
        state, rotation, translation = advance(
            state,
            rotation,
            translation,
            scalar_out,
            point_out,
            pair_out,
            w_out,
            w_hidden,
            w_back,
            w_frame,
        )
    frames = jnp.concatenate([rotation, translation], axis=0)
    return (state, frames)


def solution(mesh):
    placed = (
        P("row", "col", None),
        P(),
        P(),
        P(),
        P(("row", "col"), None),
        P(None, ("row", "col")),
        P(None, ("row", "col")),
        P(("row", "col")),
        P(("row", "col")),
        P(),
        P(),
        P(),
        P(),
        P(),
        P(),
        P(),
    )
    return jax.shard_map(
        body,
        mesh=mesh,
        in_specs=placed,
        out_specs=(P(("row", "col"), None), P(None, ("row", "col"))),
        check_vma=False,
    )
```

profile of v0, /device:TPU:8, one launch (start us, length us, event | category | flops | bytes accessed | tf_op | source)
XLA Modules:
  0.0 855.9 jit_solution(17176998492599648123)
XLA Ops:
  7.3 2.2 convolution_convert_fusion.2
  9.6 4.4 all_gather.132
  17.3 2.0 fusion.125
  19.9 4.4 all_gather.143
  24.4 4.3 all_gather.136
  30.7 40.5 %all-reduce.2 = (s32[256]{0:T(256)S(1)}, s32[256]{0:T(256)S(1)}) all-reduce(s32[256]{0:T(256)S(1)} %dynamic-update-slice.1, s32[256]{0:T(256)S(1)} %dynamic-update-slice), channel_id=1, replica_groups=mesh['row'=16,'col'=2] {'row','col'}, use_global_device_ids=true, to_apply=%add.1 | all-reduce | flops 512 | bytes 4096
  72.2 4.6 all_gather.135
  78.2 2.1 copy.358
  80.4 1.8 fusion.115
  85.9 22.8 %all-reduce.26.cloned.1.call-done = (bf16[2,192,16]{1,2,0:T(8,128)(2,1)}, bf16[2,192,16]{1,2,0:T(8,128)(2,1)}, bf16[2,192,16]{1,2,0:T(8,128)(2,1)}, bf16[2,192,1...) async-done(((bf16[2,192,16]{1,2,0:T(8,128)(2,1)}, ...) | async-done | bytes 98320 | tf_op jit(solution)/shard_map/psum | solution.py:21
  117.3 90.8 %all-reduce.20.cloned.1.call-done = (f32[144,16]{0,1:T(8,128)}, f32[144,16]{0,1:T(8,128)}, f32[144,16]{0,1:T(8,128)}, f32[144,16]{0,1:T(8,128)}, f32[144,16]{0,1...) async-done(((f32[144,16]{0,1:T(8,128)}, f32[144,16]{0,1:T(8,128)}, ...) | async-done | bytes 221200 | tf_op jit(solution)/shard_map/psum | solution.py:21
  230.5 1.7 copy.368
  235.9 4.4 all-gather.15
  240.3 4.4 all-gather.16
  247.1 6.0 all-gather.4
  253.7 5.4 all-gather
  261.5 5.8 all-gather.3
  271.0 2.5 fusion.117
  275.5 2.0 fusion.21
  277.5 2.0 convolution_bitcast_fusion.10
  280.1 4.4 all_gather.148
  284.8 4.3 all_gather.149
  289.2 4.3 all_gather.150
  293.5 4.4 all_gather.157
  301.1 91.5 %all-reduce.24.cloned.1.call-done = (bf16[2,192,16]{1,2,0:T(8,128)(2,1)}, bf16[2,192,16]{1,2,0:T(8,128)(2,1)}, bf16[2,192,16]{1,2,0:T(8,128)(2,1)}, bf16[2,192,1...) async-done(((bf16[2,192,16]{1,2,0:T(8,128)(2,1)}, ...) | async-done | bytes 98320 | tf_op jit(solution)/shard_map/psum | solution.py:21
  401.3 90.7 %all-reduce.18.cloned.1.call-done = (f32[144,16]{0,1:T(8,128)}, f32[144,16]{0,1:T(8,128)}, f32[144,16]{0,1:T(8,128)}, f32[144,16]{0,1:T(8,128)}, f32[144,16]{0,1...) async-done(((f32[144,16]{0,1:T(8,128)}, f32[144,16]{0,1:T(8,128)}, ...) | async-done | bytes 221200 | tf_op jit(solution)/shard_map/psum | solution.py:21
  505.8 4.4 all-gather.17
  510.4 4.4 all-gather.18
  517.2 6.0 all-gather.9
  523.8 5.3 all-gather.5
  542.3 1.7 copy.387
  545.3 5.8 all-gather.8
  554.8 2.5 fusion.120
  563.2 2.0 fusion.22
  565.2 2.0 convolution_bitcast_fusion.9
  567.8 4.4 all_gather.162
  572.5 4.3 all_gather.163
  576.9 4.3 all_gather.164
  581.2 4.4 all_gather.171
  588.6 91.3 %all-reduce.22.cloned.1.call-done = (bf16[2,192,16]{1,2,0:T(8,128)(2,1)}, bf16[2,192,16]{1,2,0:T(8,128)(2,1)}, bf16[2,192,16]{1,2,0:T(8,128)(2,1)}, bf16[2,192,1...) async-done(((bf16[2,192,16]{1,2,0:T(8,128)(2,1)}, ...) | async-done | bytes 98320 | tf_op jit(solution)/shard_map/psum | solution.py:21
  688.6 90.7 %all-reduce.16.cloned.1.call-done = (f32[144,16]{0,1:T(8,128)}, f32[144,16]{0,1:T(8,128)}, f32[144,16]{0,1:T(8,128)}, f32[144,16]{0,1:T(8,128)}, f32[144,16]{0,1...) async-done(((f32[144,16]{0,1:T(8,128)}, f32[144,16]{0,1:T(8,128)}, ...) | async-done | bytes 221200 | tf_op jit(solution)/shard_map/psum | solution.py:21
  793.1 4.4 all-gather.19
  799.1 4.4 all-gather.20
  804.4 5.3 all-gather.10
  811.5 5.3 all-gather.14
  828.1 1.7 copy.406
  831.2 6.0 all-gather.13
  840.2 2.5 fusion.123
  (462 shorter events, 163.3 us)
Async XLA Ops:
  7.2 263.8 %copy-start = (f32[2112,384]{1,0:T(8,128)S(1)}, f32[2112,384]{1,0:T(8,128)}, u32[]{:S(2)}) copy-start(f32[2112,384]{1,0:T(8,128)} %param.28) | copy-start | bytes 9732100
  7.2 23.0 %copy-start.66 = (s32[8]{0:T(128)S(1)}, s32[8]{0:T(128)}, u32[]{:S(2)}) copy-start(s32[8]{0:T(128)} %param.23) | copy-start | bytes 100
  7.2 23.3 %copy-start.67 = (s32[8]{0:T(128)S(1)}, s32[8]{0:T(128)}, u32[]{:S(2)}) copy-start(s32[8]{0:T(128)} %param.24) | copy-start | bytes 100
  7.2 64.3 %copy-start.68 = (f32[12]{0:T(128)S(1)}, f32[12]{0:T(128)}, u32[]{:S(2)}) copy-start(f32[12]{0:T(128)} %param.27) | copy-start | bytes 148
  7.2 73.2 %copy-start.13 = (bf16[128,128]{1,0:T(8,128)(2,1)S(1)}, bf16[128,128]{1,0:T(8,128)(2,1)}, u32[]{:S(2)}) copy-start(bf16[128,128]{1,0:T(8,128)(2,1)} %param.17) | copy-start | bytes 98308
  7.2 101.5 %all-reduce.26.cloned.1.call-start = ((), (), s32[]{:S(2)}) async-start(), calls=%async_computation.5 | async-start | bytes 262144 | tf_op jit(solution)/shard_map/psum | solution.py:21
  14.6 68.8 %copy-start.65 = (f32[128]{0:T(128)S(1)}, f32[128]{0:T(128)}, u32[]{:S(2)}) copy-start(f32[128]{0:T(128)} %param.18) | copy-start | bytes 1540
  14.7 193.5 %all-reduce.20.cloned.1.call-start = ((), (), s32[]{:S(2)}) async-start(), calls=%async_computation.2 | async-start | bytes 655360 | tf_op jit(solution)/shard_map/psum | solution.py:21
  17.1 7.2 copy-start.55
  17.1 7.2 copy-start.56
  17.1 7.2 copy-start.57
  17.3 7.0 copy-start.54
  28.8 56.9 %copy-start.64 = (bf16[128,12]{0,1:T(8,128)(2,1)S(1)}, bf16[128,12]{0,1:T(8,128)(2,1)}, u32[]{:S(2)}) copy-start(bf16[128,12]{0,1:T(8,128)(2,1)} %param.19) | copy-start | bytes 9220
  30.1 362.5 %all-reduce.24.cloned.1.call-start = ((), (), s32[]{:S(2)}) async-start(), calls=%async_computation.4 | async-start | bytes 262144 | tf_op jit(solution)/shard_map/psum | solution.py:21
  80.4 151.8 %copy-start.60 = (f32[12]{0:T(128)S(1)}, f32[12]{0:T(128)}, u32[]{:S(2)}) copy-start(f32[12]{0:T(128)} %fusion.102) | copy-start | bytes 148
  83.4 152.5 %copy-start.11 = (pred[16,128]{1,0:T(8,128)(4,1)}, pred[16,128]{1,0:T(8,128)(4,1)S(1)}, u32[]{:S(2)}) copy-start(pred[16,128]{1,0:T(8,128)(4,1)S(1)} %broadcast_and_fusion) | copy-start | bytes 6148
  268.2 6.8 copy-start.44
  275.2 9.3 %copy-start.39 = (f32[1,8]{1,0:T(1,128)}, f32[1,8]{1,0:T(1,128)S(1)}, u32[]{:S(2)}) copy-start(f32[1,8]{1,0:T(1,128)S(1)} %get-tuple-element.382) | copy-start | bytes 100
  275.2 9.4 %copy-start.40 = (f32[1,8]{1,0:T(1,128)}, f32[1,8]{1,0:T(1,128)S(1)}, u32[]{:S(2)}) copy-start(f32[1,8]{1,0:T(1,128)S(1)} %get-tuple-element.381) | copy-start | bytes 100
  275.3 9.2 %copy-start.38 = (f32[1,8]{1,0:T(1,128)}, f32[1,8]{1,0:T(1,128)S(1)}, u32[]{:S(2)}) copy-start(f32[1,8]{1,0:T(1,128)S(1)} %get-tuple-element.468) | copy-start | bytes 100
  275.4 9.1 %copy-start.37 = (f32[1,8]{1,0:T(1,128)}, f32[1,8]{1,0:T(1,128)S(1)}, u32[]{:S(2)}) copy-start(f32[1,8]{1,0:T(1,128)S(1)} %get-tuple-element.361) | copy-start | bytes 100
  275.4 9.1 %copy-start.36 = (f32[1,8]{1,0:T(1,128)}, f32[1,8]{1,0:T(1,128)S(1)}, u32[]{:S(2)}) copy-start(f32[1,8]{1,0:T(1,128)S(1)} %get-tuple-element.360) | copy-start | bytes 100
  275.5 9.3 %copy-start.14 = (f32[1,8]{1,0:T(1,128)}, f32[1,8]{1,0:T(1,128)S(1)}, u32[]{:S(2)}) copy-start(f32[1,8]{1,0:T(1,128)S(1)} %get-tuple-element.364) | copy-start | bytes 100
  300.0 192.0 %all-reduce.18.cloned.1.call-start = ((), (), s32[]{:S(2)}) async-start(), calls=%async_computation.1 | async-start | bytes 655360 | tf_op jit(solution)/shard_map/psum | solution.py:21
  301.1 378.8 %all-reduce.22.cloned.1.call-start = ((), (), s32[]{:S(2)}) async-start(), calls=%async_computation.3 | async-start | bytes 262144 | tf_op jit(solution)/shard_map/psum | solution.py:21
  505.8 46.3 %copy-start.15 = (f32[1,8]{1,0:T(1,128)S(1)}, f32[1,8]{1,0:T(1,128)}, u32[]{:S(2)}) copy-start(f32[1,8]{1,0:T(1,128)} %copy-done.14) | copy-start | bytes 100
  529.2 22.0 %copy-start.9 = (f32[12,8]{1,0:T(8,128)}, f32[12,8]{1,0:T(8,128)S(1)}, u32[]{:S(2)}) copy-start(f32[12,8]{1,0:T(8,128)S(1)} %get-tuple-element.421) | copy-start | bytes 1156
  552.0 6.7 copy-start.45
  558.0 234.0 %copy-start.12 = (pred[16,128]{1,0:T(8,128)(4,1)S(1)}, pred[16,128]{1,0:T(8,128)(4,1)}, u32[]{:S(2)}) copy-start(pred[16,128]{1,0:T(8,128)(4,1)} %copy-done.11) | copy-start | bytes 6148
  558.5 13.7 %copy-start.58 = (f32[8]{0:T(128)}, f32[8]{0:T(128)S(1)}, u32[]{:S(2)}) copy-start(f32[8]{0:T(128)S(1)} %broadcast_multiply_fusion.7) | copy-start | bytes 100
  558.7 8.5 copy-start.62
  559.6 7.8 copy-start.41
  560.3 11.9 %copy-start.42 = (f32[1,8]{1,0:T(1,128)}, f32[1,8]{1,0:T(1,128)S(1)}, u32[]{:S(2)}) copy-start(f32[1,8]{1,0:T(1,128)S(1)} %get-tuple-element.447) | copy-start | bytes 100
  561.0 11.2 %copy-start.43 = (f32[1,8]{1,0:T(1,128)}, f32[1,8]{1,0:T(1,128)S(1)}, u32[]{:S(2)}) copy-start(f32[1,8]{1,0:T(1,128)S(1)} %get-tuple-element.452) | copy-start | bytes 100
  561.8 5.8 copy-start.18
  561.8 5.8 copy-start.20
  561.8 10.6 %copy-start.22 = (f32[1,8]{1,0:T(1,128)}, f32[1,8]{1,0:T(1,128)S(1)}, u32[]{:S(2)}) copy-start(f32[1,8]{1,0:T(1,128)S(1)} %get-tuple-element.409) | copy-start | bytes 100
  562.5 9.9 %copy-start.26 = (f32[1,8]{1,0:T(1,128)}, f32[1,8]{1,0:T(1,128)S(1)}, u32[]{:S(2)}) copy-start(f32[1,8]{1,0:T(1,128)S(1)} %get-tuple-element.410) | copy-start | bytes 100
  562.5 9.9 %copy-start.28 = (f32[1,8]{1,0:T(1,128)}, f32[1,8]{1,0:T(1,128)S(1)}, u32[]{:S(2)}) copy-start(f32[1,8]{1,0:T(1,128)S(1)} %get-tuple-element.411) | copy-start | bytes 100
  562.5 9.9 %copy-start.30 = (f32[1,8]{1,0:T(1,128)}, f32[1,8]{1,0:T(1,128)S(1)}, u32[]{:S(2)}) copy-start(f32[1,8]{1,0:T(1,128)S(1)} %get-tuple-element.412) | copy-start | bytes 100
  563.2 9.0 %copy-start.33 = (f32[1,8]{1,0:T(1,128)}, f32[1,8]{1,0:T(1,128)S(1)}, u32[]{:S(2)}) copy-start(f32[1,8]{1,0:T(1,128)S(1)} %get-tuple-element.415) | copy-start | bytes 100
  587.7 191.6 %all-reduce.16.cloned.1.call-start = ((), (), s32[]{:S(2)}) async-start(), calls=%async_computation | async-start | bytes 655360 | tf_op jit(solution)/shard_map/psum | solution.py:21
  793.0 45.2 %copy-start.19 = (f32[1,8]{1,0:T(1,128)S(1)}, f32[1,8]{1,0:T(1,128)}, u32[]{:S(2)}) copy-start(f32[1,8]{1,0:T(1,128)} %copy-done.18) | copy-start | bytes 100
  793.0 45.2 %copy-start.21 = (f32[1,8]{1,0:T(1,128)S(1)}, f32[1,8]{1,0:T(1,128)}, u32[]{:S(2)}) copy-start(f32[1,8]{1,0:T(1,128)} %copy-done.20) | copy-start | bytes 100
  793.1 45.2 %copy-start.23 = (f32[1,8]{1,0:T(1,128)S(1)}, f32[1,8]{1,0:T(1,128)}, u32[]{:S(2)}) copy-start(f32[1,8]{1,0:T(1,128)} %copy-done.22) | copy-start | bytes 100
  837.2 8.4 copy-start.27
  837.2 8.4 copy-start.29
  844.2 4.9 copy-start.10
  (27 other events, 89.3 us)
Sparse Core Ops, SparseCore 0:
  14.8 93.8 all-reduce.25
  113.9 94.2 all-reduce.19
  300.2 92.4 all-reduce.23
  397.7 94.3 all-reduce.17
  587.9 91.9 all-reduce.21
  685.0 94.3 all-reduce.15
where the time goes:
time: 862 us; the launch traced here: 856 us
  waiting for transfers between devices  478 us (55%)
  blocking collectives  170 us (20%)
  local copies, waits for them, and re-layouts  119 us (14%)
  matrix products  43.3 us (5%)
  other arithmetic  29.7 us (3%)
  between operations  15.7 us (2%)
    psum x6, waiting for transfers between devices, broadcast(): return lax.psum(jnp.where(mine, value, jnp.zeros_like(value)), axis)  478 us
    all_gather x15, blocking collectives, joined(): gathered = jax.tree.map(lambda a: lax.all_gather(a, axis), part)  77 us
    unnamed x207, local copies, waits for them, and re-layouts  76.3 us
    unnamed x1, blocking collectives  40.5 us
  transfers between devices with their start and end apart: 6, of which 6 were waited for; matrix products, arithmetic and copies ran while one was open for 5% of the time, Pallas kernels for 0%

commit v1 on v0

--- a/solution.py
+++ b/solution.py
@@ -18,7 +18,7 @@
 
 def broadcast(value, axis, root):
     mine = lax.axis_index(axis) == root
-    return lax.psum(jnp.where(mine, value, jnp.zeros_like(value)), axis)
+    return jnp.sum(lax.all_gather(jnp.where(mine, value, jnp.zeros_like(value)), axis), axis=0)
 
 
 def joined(part, axis, combine):

time: 862 us -> 1920 us (2.23)
  blocking collectives: 170 us -> 1620 us
  waiting for transfers between devices: 478 us -> 0 us
  other arithmetic: 29.7 us -> 116 us
    all_gather x0 -> x72, blocking collectives: none -> 1450 us  [broadcast(): lax.all_gather(jnp.where(mine, value, jnp.zeros_like(value)), axis)]
    psum x6 -> x0, waiting for transfers between devices: 478 us -> none  [broadcast(): return lax.psum(jnp.where(mine, value, jnp.zeros_like(value)), axis)]
    reduce_sum x0 -> x72, other arithmetic: none -> 79.8 us  [broadcast(): jnp.sum(lax.all_gather(jnp.where(mine, value, jnp.zeros_like(value)), axi...]
    unnamed x207 -> x259, local copies, waits for them, and re-layouts: 76.3 us -> 69.6 us
  transfers between devices with their start and end apart: 6 -> 0, of which waited for: 6 -> 0; matrix products, arithmetic and copies ran while one was open for 5% -> 0% of each run, Pallas kernels for 0% -> 0%
where the time goes in v1:
time: 1920 us; the launch traced here: 1900 us
  blocking collectives  1620 us (84%)
  local copies, waits for them, and re-layouts  116 us (6%)
  other arithmetic  116 us (6%)
  matrix products  44.2 us (2%)
    all_gather x72, blocking collectives, broadcast(): lax.all_gather(jnp.where(mine, value, jnp.zeros_like(value)), axis)  1450 us
    reduce_sum x72, other arithmetic, broadcast(): jnp.sum(lax.all_gather(jnp.where(mine, value, jnp.zeros_like(value)), axi...  79.8 us
    all_gather x15, blocking collectives, joined(): gathered = jax.tree.map(lambda a: lax.all_gather(a, axis), part)  79.3 us
    unnamed x259, local copies, waits for them, and re-layouts  69.6 us
    unnamed x1, blocking collectives  41.9 us

profile of v1, /device:TPU:8, one launch (start us, length us, event | category | flops | bytes accessed | tf_op | source)
XLA Modules:
  0.0 1900.4 jit_solution(11338362409022594309)
XLA Ops:
  53.7 19.7 %all-gather.89 = f32[16,144,16]{1,2,0:T(8,128)S(1)} all-gather(f32[1,144,16]{1,2,0:T(8,128)} %get-tuple-element.306), channel_id=12, replica_groups=mesh['row'=16,'col'=2] {'row'}, dimensions={0}, use_global_device_ids=true | all-gather | bytes 156672 | tf_op jit(solution)/shard_map/all_gather | solution.py:21
  95.7 19.7 %all-gather.91 = f32[16,144,16]{1,2,0:T(8,128)S(1)} all-gather(f32[1,144,16]{1,2,0:T(8,128)} %get-tuple-element.304), channel_id=14, replica_groups=mesh['row'=16,'col'=2] {'row'}, dimensions={0}, use_global_device_ids=true | all-gather | bytes 156672 | tf_op jit(solution)/shard_map/all_gather | solution.py:21
  137.6 19.7 %all-gather.93 = f32[16,144,16]{1,2,0:T(8,128)S(1)} all-gather(f32[1,144,16]{1,2,0:T(8,128)} %get-tuple-element.302), channel_id=16, replica_groups=mesh['row'=16,'col'=2] {'row'}, dimensions={0}, use_global_device_ids=true | all-gather | bytes 156672 | tf_op jit(solution)/shard_map/all_gather | solution.py:21
  235.0 19.7 %all-gather.2 = bf16[32,192,16]{1,2,0:T(8,128)(2,1)S(1)} all-gather(bf16[2,192,16]{1,2,0:T(8,128)(2,1)} %get-tuple-element.234), channel_id=4, replica_groups=mesh['row'=16,'col'=2] {'row'}, dimensions={0}, use_global_device_ids=true | all-gather | bytes 208896 | tf_op jit(solution)/shard_map/all_gather | solution.py:21
  277.0 19.6 %all-gather.4 = bf16[32,192,16]{1,2,0:T(8,128)(2,1)S(1)} all-gather(bf16[2,192,16]{1,2,0:T(8,128)(2,1)} %get-tuple-element.236), channel_id=6, replica_groups=mesh['row'=16,'col'=2] {'row'}, dimensions={0}, use_global_device_ids=true | all-gather | bytes 208896 | tf_op jit(solution)/shard_map/all_gather | solution.py:21
  364.7 41.9 %all-reduce.2 = (s32[256]{0:T(256)S(1)}, s32[256]{0:T(256)S(1)}) all-reduce(s32[256]{0:T(256)S(1)} %dynamic-update-slice.1, s32[256]{0:T(256)S(1)} %dynamic-update-slice), channel_id=1, replica_groups=mesh['row'=16,'col'=2] {'row','col'}, use_global_device_ids=true, to_apply=%add.1 | all-reduce | flops 512 | bytes 4096
  464.7 20.1 %all-gather.98 = f32[16,288,16]{1,2,0:T(8,128)} all-gather(f32[1,288,16]{1,2,0:T(8,128)} %get-tuple-element.230), channel_id=22, replica_groups=mesh['row'=16,'col'=2] {'row'}, dimensions={0}, use_global_device_ids=true | all-gather | bytes 313344 | tf_op jit(solution)/shard_map/all_gather | solution.py:21
  487.8 21.5 %all-gather.99 = f32[16,288,16]{1,2,0:T(8,128)} all-gather(f32[1,288,16]{1,2,0:T(8,128)} %get-tuple-element.229), channel_id=23, replica_groups=mesh['row'=16,'col'=2] {'row'}, dimensions={0}, use_global_device_ids=true | all-gather | bytes 313344 | tf_op jit(solution)/shard_map/all_gather | solution.py:21
  512.2 19.9 %all-gather.100 = f32[16,288,16]{1,2,0:T(8,128)} all-gather(f32[1,288,16]{1,2,0:T(8,128)S(1)} %get-tuple-element.228), channel_id=24, replica_groups=mesh['row'=16,'col'=2] {'row'}, dimensions={0}, use_global_device_ids=true | all-gather | bytes 313344 | tf_op jit(solution)/shard_map/all_gather | solution.py:21
  533.8 21.6 %all-gather.101 = f32[16,288,16]{1,2,0:T(8,128)} all-gather(f32[1,288,16]{1,2,0:T(8,128)} %get-tuple-element.227), channel_id=25, replica_groups=mesh['row'=16,'col'=2] {'row'}, dimensions={0}, use_global_device_ids=true | all-gather | bytes 313344 | tf_op jit(solution)/shard_map/all_gather | solution.py:21
  558.4 20.1 %all-gather.102 = f32[16,288,16]{1,2,0:T(8,128)} all-gather(f32[1,288,16]{1,2,0:T(8,128)} %get-tuple-element.226), channel_id=26, replica_groups=mesh['row'=16,'col'=2] {'row'}, dimensions={0}, use_global_device_ids=true | all-gather | bytes 313344 | tf_op jit(solution)/shard_map/all_gather | solution.py:21
  581.5 22.0 %all-gather.103 = f32[16,288,16]{1,2,0:T(8,128)} all-gather(f32[1,288,16]{1,2,0:T(8,128)} %get-tuple-element.225), channel_id=27, replica_groups=mesh['row'=16,'col'=2] {'row'}, dimensions={0}, use_global_device_ids=true | all-gather | bytes 313344 | tf_op jit(solution)/shard_map/all_gather | solution.py:21
  606.5 20.1 %all-gather.104 = f32[16,288,16]{1,2,0:T(8,128)} all-gather(f32[1,288,16]{1,2,0:T(8,128)} %get-tuple-element.224), channel_id=28, replica_groups=mesh['row'=16,'col'=2] {'row'}, dimensions={0}, use_global_device_ids=true | all-gather | bytes 313344 | tf_op jit(solution)/shard_map/all_gather | solution.py:21
  669.9 20.9 %all-gather.105 = f32[16,144,16]{1,2,0:T(8,128)} all-gather(f32[1,144,16]{1,2,0:T(8,128)S(1)} %get-tuple-element.287), channel_id=39, replica_groups=mesh['row'=16,'col'=2] {'row'}, dimensions={0}, use_global_device_ids=true | all-gather | bytes 156672 | tf_op jit(solution)/shard_map/all_gather | solution.py:21
  692.4 19.7 %all-gather.106 = f32[16,144,16]{1,2,0:T(8,128)} all-gather(f32[1,144,16]{1,2,0:T(8,128)S(1)} %get-tuple-element.286), channel_id=40, replica_groups=mesh['row'=16,'col'=2] {'row'}, dimensions={0}, use_global_device_ids=true | all-gather | bytes 156672 | tf_op jit(solution)/shard_map/all_gather | solution.py:21
  713.6 20.9 %all-gather.107 = f32[16,144,16]{1,2,0:T(8,128)} all-gather(f32[1,144,16]{1,2,0:T(8,128)S(1)} %get-tuple-element.285), channel_id=41, replica_groups=mesh['row'=16,'col'=2] {'row'}, dimensions={0}, use_global_device_ids=true | all-gather | bytes 156672 | tf_op jit(solution)/shard_map/all_gather | solution.py:21
  757.2 20.9 %all-gather.109 = f32[16,144,16]{1,2,0:T(8,128)} all-gather(f32[1,144,16]{1,2,0:T(8,128)S(1)} %get-tuple-element.283), channel_id=43, replica_groups=mesh['row'=16,'col'=2] {'row'}, dimensions={0}, use_global_device_ids=true | all-gather | bytes 156672 | tf_op jit(solution)/shard_map/all_gather | solution.py:21
  800.7 20.9 %all-gather.111 = f32[16,144,16]{1,2,0:T(8,128)} all-gather(f32[1,144,16]{1,2,0:T(8,128)S(1)} %get-tuple-element.281), channel_id=45, replica_groups=mesh['row'=16,'col'=2] {'row'}, dimensions={0}, use_global_device_ids=true | all-gather | bytes 156672 | tf_op jit(solution)/shard_map/all_gather | solution.py:21
  859.9 20.9 %all-gather.29 = bf16[32,192,16]{1,2,0:T(8,128)(2,1)} all-gather(bf16[2,192,16]{1,2,0:T(8,128)(2,1)S(1)} %get-tuple-element.223), channel_id=31, replica_groups=mesh['row'=16,'col'=2] {'row'}, dimensions={0}, use_global_device_ids=true | all-gather | bytes 208896 | tf_op jit(solution)/shard_map/all_gather | solution.py:21
  904.9 20.9 %all-gather.31 = bf16[32,192,16]{1,2,0:T(8,128)(2,1)} all-gather(bf16[2,192,16]{1,2,0:T(8,128)(2,1)S(1)} %get-tuple-element.218), channel_id=33, replica_groups=mesh['row'=16,'col'=2] {'row'}, dimensions={0}, use_global_device_ids=true | all-gather | bytes 208896 | tf_op jit(solution)/shard_map/all_gather | solution.py:21
  948.5 20.9 %all-gather.33 = bf16[32,192,16]{1,2,0:T(8,128)(2,1)} all-gather(bf16[2,192,16]{1,2,0:T(8,128)(2,1)S(1)} %get-tuple-element.220), channel_id=35, replica_groups=mesh['row'=16,'col'=2] {'row'}, dimensions={0}, use_global_device_ids=true | all-gather | bytes 208896 | tf_op jit(solution)/shard_map/all_gather | solution.py:21
  992.1 20.9 %all-gather.35 = bf16[32,192,16]{1,2,0:T(8,128)(2,1)} all-gather(bf16[2,192,16]{1,2,0:T(8,128)(2,1)S(1)} %get-tuple-element.222), channel_id=37, replica_groups=mesh['row'=16,'col'=2] {'row'}, dimensions={0}, use_global_device_ids=true | all-gather | bytes 208896 | tf_op jit(solution)/shard_map/all_gather | solution.py:21
  1065.1 21.4 %all-gather.115 = f32[16,288,16]{1,2,0:T(8,128)} all-gather(f32[1,288,16]{1,2,0:T(8,128)S(1)} %get-tuple-element.215), channel_id=50, replica_groups=mesh['row'=16,'col'=2] {'row'}, dimensions={0}, use_global_device_ids=true | all-gather | bytes 313344 | tf_op jit(solution)/shard_map/all_gather | solution.py:21
  1089.4 20.1 %all-gather.116 = f32[16,288,16]{1,2,0:T(8,128)} all-gather(f32[1,288,16]{1,2,0:T(8,128)} %get-tuple-element.214), channel_id=51, replica_groups=mesh['row'=16,'col'=2] {'row'}, dimensions={0}, use_global_device_ids=true | all-gather | bytes 313344 | tf_op jit(solution)/shard_map/all_gather | solution.py:21
  1112.6 21.5 %all-gather.117 = f32[16,288,16]{1,2,0:T(8,128)} all-gather(f32[1,288,16]{1,2,0:T(8,128)} %get-tuple-element.213), channel_id=52, replica_groups=mesh['row'=16,'col'=2] {'row'}, dimensions={0}, use_global_device_ids=true | all-gather | bytes 313344 | tf_op jit(solution)/shard_map/all_gather | solution.py:21
  1137.1 20.1 %all-gather.118 = f32[16,288,16]{1,2,0:T(8,128)} all-gather(f32[1,288,16]{1,2,0:T(8,128)} %get-tuple-element.212), channel_id=53, replica_groups=mesh['row'=16,'col'=2] {'row'}, dimensions={0}, use_global_device_ids=true | all-gather | bytes 313344 | tf_op jit(solution)/shard_map/all_gather | solution.py:21
  1160.2 21.5 %all-gather.119 = f32[16,288,16]{1,2,0:T(8,128)} all-gather(f32[1,288,16]{1,2,0:T(8,128)} %get-tuple-element.211), channel_id=54, replica_groups=mesh['row'=16,'col'=2] {'row'}, dimensions={0}, use_global_device_ids=true | all-gather | bytes 313344 | tf_op jit(solution)/shard_map/all_gather | solution.py:21
  1184.7 20.1 %all-gather.120 = f32[16,288,16]{1,2,0:T(8,128)} all-gather(f32[1,288,16]{1,2,0:T(8,128)} %get-tuple-element.210), channel_id=55, replica_groups=mesh['row'=16,'col'=2] {'row'}, dimensions={0}, use_global_device_ids=true | all-gather | bytes 313344 | tf_op jit(solution)/shard_map/all_gather | solution.py:21
  1207.8 21.5 %all-gather.121 = f32[16,288,16]{1,2,0:T(8,128)} all-gather(f32[1,288,16]{1,2,0:T(8,128)} %get-tuple-element.209), channel_id=56, replica_groups=mesh['row'=16,'col'=2] {'row'}, dimensions={0}, use_global_device_ids=true | all-gather | bytes 313344 | tf_op jit(solution)/shard_map/all_gather | solution.py:21
  1232.3 20.1 %all-gather.122 = f32[16,288,16]{1,2,0:T(8,128)} all-gather(f32[1,288,16]{1,2,0:T(8,128)} %get-tuple-element.208), channel_id=57, replica_groups=mesh['row'=16,'col'=2] {'row'}, dimensions={0}, use_global_device_ids=true | all-gather | bytes 313344 | tf_op jit(solution)/shard_map/all_gather | solution.py:21
  1295.3 20.9 %all-gather.123 = f32[16,144,16]{1,2,0:T(8,128)} all-gather(f32[1,144,16]{1,2,0:T(8,128)S(1)} %get-tuple-element.275), channel_id=68, replica_groups=mesh['row'=16,'col'=2] {'row'}, dimensions={0}, use_global_device_ids=true | all-gather | bytes 156672 | tf_op jit(solution)/shard_map/all_gather | solution.py:21
  1317.8 19.7 %all-gather.124 = f32[16,144,16]{1,2,0:T(8,128)} all-gather(f32[1,144,16]{1,2,0:T(8,128)S(1)} %get-tuple-element.274), channel_id=69, replica_groups=mesh['row'=16,'col'=2] {'row'}, dimensions={0}, use_global_device_ids=true | all-gather | bytes 156672 | tf_op jit(solution)/shard_map/all_gather | solution.py:21
  1339.1 20.9 %all-gather.125 = f32[16,144,16]{1,2,0:T(8,128)} all-gather(f32[1,144,16]{1,2,0:T(8,128)S(1)} %get-tuple-element.273), channel_id=70, replica_groups=mesh['row'=16,'col'=2] {'row'}, dimensions={0}, use_global_device_ids=true | all-gather | bytes 156672 | tf_op jit(solution)/shard_map/all_gather | solution.py:21
  1382.6 20.9 %all-gather.127 = f32[16,144,16]{1,2,0:T(8,128)} all-gather(f32[1,144,16]{1,2,0:T(8,128)S(1)} %get-tuple-element.271), channel_id=72, replica_groups=mesh['row'=16,'col'=2] {'row'}, dimensions={0}, use_global_device_ids=true | all-gather | bytes 156672 | tf_op jit(solution)/shard_map/all_gather | solution.py:21
  1426.2 20.9 %all-gather.129 = f32[16,144,16]{1,2,0:T(8,128)} all-gather(f32[1,144,16]{1,2,0:T(8,128)S(1)} %get-tuple-element.269), channel_id=74, replica_groups=mesh['row'=16,'col'=2] {'row'}, dimensions={0}, use_global_device_ids=true | all-gather | bytes 156672 | tf_op jit(solution)/shard_map/all_gather | solution.py:21
  1485.3 20.9 %all-gather.58 = bf16[32,192,16]{1,2,0:T(8,128)(2,1)} all-gather(bf16[2,192,16]{1,2,0:T(8,128)(2,1)S(1)} %get-tuple-element.207), channel_id=60, replica_groups=mesh['row'=16,'col'=2] {'row'}, dimensions={0}, use_global_device_ids=true | all-gather | bytes 208896 | tf_op jit(solution)/shard_map/all_gather | solution.py:21
  1530.3 20.9 %all-gather.60 = bf16[32,192,16]{1,2,0:T(8,128)(2,1)} all-gather(bf16[2,192,16]{1,2,0:T(8,128)(2,1)S(1)} %get-tuple-element.202), channel_id=62, replica_groups=mesh['row'=16,'col'=2] {'row'}, dimensions={0}, use_global_device_ids=true | all-gather | bytes 208896 | tf_op jit(solution)/shard_map/all_gather | solution.py:21
  1573.9 20.9 %all-gather.62 = bf16[32,192,16]{1,2,0:T(8,128)(2,1)} all-gather(bf16[2,192,16]{1,2,0:T(8,128)(2,1)S(1)} %get-tuple-element.204), channel_id=64, replica_groups=mesh['row'=16,'col'=2] {'row'}, dimensions={0}, use_global_device_ids=true | all-gather | bytes 208896 | tf_op jit(solution)/shard_map/all_gather | solution.py:21
  1617.5 20.9 %all-gather.64 = bf16[32,192,16]{1,2,0:T(8,128)(2,1)} all-gather(bf16[2,192,16]{1,2,0:T(8,128)(2,1)S(1)} %get-tuple-element.206), channel_id=66, replica_groups=mesh['row'=16,'col'=2] {'row'}, dimensions={0}, use_global_device_ids=true | all-gather | bytes 208896 | tf_op jit(solution)/shard_map/all_gather | solution.py:21
  1640.0 19.7 %all-gather.65 = bf16[32,192,16]{1,2,0:T(8,128)(2,1)} all-gather(bf16[2,192,16]{1,2,0:T(8,128)(2,1)S(1)} %get-tuple-element.200), channel_id=67, replica_groups=mesh['row'=16,'col'=2] {'row'}, dimensions={0}, use_global_device_ids=true | all-gather | bytes 208896 | tf_op jit(solution)/shard_map/all_gather | solution.py:21
  1689.2 21.2 %all-gather.133 = f32[16,288,16]{1,2,0:T(8,128)} all-gather(f32[1,288,16]{1,2,0:T(8,128)S(1)} %get-tuple-element.199), channel_id=79, replica_groups=mesh['row'=16,'col'=2] {'row'}, dimensions={0}, use_global_device_ids=true | all-gather | bytes 313344 | tf_op jit(solution)/shard_map/all_gather | solution.py:21
  1713.4 20.3 %all-gather.134 = f32[16,288,16]{1,2,0:T(8,128)} all-gather(f32[1,288,16]{1,2,0:T(8,128)} %get-tuple-element.198), channel_id=80, replica_groups=mesh['row'=16,'col'=2] {'row'}, dimensions={0}, use_global_device_ids=true | all-gather | bytes 313344 | tf_op jit(solution)/shard_map/all_gather | solution.py:21
  1736.6 21.5 %all-gather.135 = f32[16,288,16]{1,2,0:T(8,128)} all-gather(f32[1,288,16]{1,2,0:T(8,128)} %get-tuple-element.197), channel_id=81, replica_groups=mesh['row'=16,'col'=2] {'row'}, dimensions={0}, use_global_device_ids=true | all-gather | bytes 313344 | tf_op jit(solution)/shard_map/all_gather | solution.py:21
  1761.1 20.1 %all-gather.136 = f32[16,288,16]{1,2,0:T(8,128)} all-gather(f32[1,288,16]{1,2,0:T(8,128)} %get-tuple-element.196), channel_id=82, replica_groups=mesh['row'=16,'col'=2] {'row'}, dimensions={0}, use_global_device_ids=true | all-gather | bytes 313344 | tf_op jit(solution)/shard_map/all_gather | solution.py:21
  1784.2 21.5 %all-gather.137 = f32[16,288,16]{1,2,0:T(8,128)} all-gather(f32[1,288,16]{1,2,0:T(8,128)} %get-tuple-element.195), channel_id=83, replica_groups=mesh['row'=16,'col'=2] {'row'}, dimensions={0}, use_global_device_ids=true | all-gather | bytes 313344 | tf_op jit(solution)/shard_map/all_gather | solution.py:21
  1808.7 20.1 %all-gather.138 = f32[16,288,16]{1,2,0:T(8,128)} all-gather(f32[1,288,16]{1,2,0:T(8,128)} %get-tuple-element.194), channel_id=84, replica_groups=mesh['row'=16,'col'=2] {'row'}, dimensions={0}, use_global_device_ids=true | all-gather | bytes 313344 | tf_op jit(solution)/shard_map/all_gather | solution.py:21
  1831.8 21.3 %all-gather.139 = f32[16,288,16]{1,2,0:T(8,128)} all-gather(f32[1,288,16]{1,2,0:T(8,128)S(1)} %get-tuple-element.193), channel_id=85, replica_groups=mesh['row'=16,'col'=2] {'row'}, dimensions={0}, use_global_device_ids=true | all-gather | bytes 313344 | tf_op jit(solution)/shard_map/all_gather | solution.py:21
  1854.7 19.9 %all-gather.140 = f32[16,288,16]{1,2,0:T(8,128)} all-gather(f32[1,288,16]{1,2,0:T(8,128)S(1)} %get-tuple-element.192), channel_id=86, replica_groups=mesh['row'=16,'col'=2] {'row'}, dimensions={0}, use_global_device_ids=true | all-gather | bytes 313344 | tf_op jit(solution)/shard_map/all_gather | solution.py:21
  (640 shorter events, 886.4 us)
Async XLA Ops:
  0.6 651.8 %copy-start = (f32[2112,384]{1,0:T(8,128)S(1)}, f32[2112,384]{1,0:T(8,128)}, u32[]{:S(2)}) copy-start(f32[2112,384]{1,0:T(8,128)} %param.28) | copy-start | bytes 9732100
  2.5 9.4 copy-start.77
  2.5 9.4 copy-start.78
  2.5 9.4 copy-start.79
  2.5 9.3 copy-start.82
  2.5 9.3 copy-start.84
  3.0 183.0 %copy-start.22 = (f32[8,384]{1,0:T(8,128)S(1)}, f32[8,384]{1,0:T(8,128)}, u32[]{:S(2)}) copy-start(f32[8,384]{1,0:T(8,128)} %param.20) | copy-start | bytes 36868
  185.0 8.2 copy-start.90
  186.0 177.7 %copy-start.94 = (s32[8]{0:T(128)S(1)}, s32[8]{0:T(128)}, u32[]{:S(2)}) copy-start(s32[8]{0:T(128)} %param.24) | copy-start | bytes 100
  410.8 25.0 %copy-start.76 = (f32[8]{0:T(128)S(1)}, f32[8]{0:T(128)}, u32[]{:S(2)}) copy-start(f32[8]{0:T(128)} %copy-done.75) | copy-start | bytes 100
  413.7 9.8 copy-start.25
  415.6 118.2 %copy-start.20 = (f32[12,16]{1,0:T(8,128)}, f32[12,16]{1,0:T(8,128)S(1)}, u32[]{:S(2)}) copy-start(f32[12,16]{1,0:T(8,128)S(1)} %get-tuple-element.414) | copy-start | bytes 2308
  533.8 111.2 %copy-start.9 = (bf16[12,16,128]{2,1,0:T(8,128)(2,1)S(1)}, bf16[12,16,128]{2,1,0:T(8,128)(2,1)}, u32[]{:S(2)}) copy-start(bf16[12,16,128]{2,1,0:T(8,128)(2,1)} %copy-done.8) | copy-start | bytes 147460
  645.9 10.5 copy-start.72
  656.5 9.0 copy-start.93
  669.9 175.4 %copy-start.60 = (f32[1,48,8]{1,2,0:T(8,128)S(1)}, f32[1,48,8]{1,2,0:T(8,128)}, u32[]{:S(2)}) copy-start(f32[1,48,8]{1,2,0:T(8,128)} %get-tuple-element.247) | copy-start | bytes 4612
  669.9 175.4 %copy-start.61 = (f32[1,48,8]{1,2,0:T(8,128)S(1)}, f32[1,48,8]{1,2,0:T(8,128)}, u32[]{:S(2)}) copy-start(f32[1,48,8]{1,2,0:T(8,128)} %get-tuple-element.249) | copy-start | bytes 4612
  692.4 153.0 %copy-start.62 = (f32[1,48,8]{1,2,0:T(8,128)S(1)}, f32[1,48,8]{1,2,0:T(8,128)}, u32[]{:S(2)}) copy-start(f32[1,48,8]{1,2,0:T(8,128)} %get-tuple-element.251) | copy-start | bytes 4612
  1040.6 18.5 copy-start.21
  1134.1 131.2 %copy-start.14 = (f32[12,8]{1,0:T(8,128)S(1)}, f32[12,8]{1,0:T(8,128)}, u32[]{:S(2)}) copy-start(f32[12,8]{1,0:T(8,128)} %copy-done.13) | copy-start | bytes 1156
  1134.1 131.2 %copy-start.16 = (f32[12,8]{1,0:T(8,128)S(1)}, f32[12,8]{1,0:T(8,128)}, u32[]{:S(2)}) copy-start(f32[12,8]{1,0:T(8,128)} %copy-done.15) | copy-start | bytes 1156
  1158.9 110.1 %copy-start.27 = (f32[1,8]{1,0:T(1,128)S(1)}, f32[1,8]{1,0:T(1,128)}, u32[]{:S(2)}) copy-start(f32[1,8]{1,0:T(1,128)} %copy-done.26) | copy-start | bytes 100
  1279.0 11.0 copy-start.30
  1279.0 11.0 copy-start.49
  1279.0 11.0 copy-start.57
  1279.0 11.2 copy-start.28
  1279.0 11.2 copy-start.39
  1279.0 11.2 copy-start.41
  1284.6 194.2 %copy-start.88 = (f32[8]{0:T(128)}, f32[8]{0:T(128)S(1)}, u32[]{:S(2)}) copy-start(f32[8]{0:T(128)S(1)} %broadcast_multiply_fusion.7) | copy-start | bytes 100
  1317.8 161.0 %copy-start.92 = (f32[8]{0:T(128)S(1)}, f32[8]{0:T(128)}, u32[]{:S(2)}) copy-start(f32[8]{0:T(128)} %copy-done.91) | copy-start | bytes 100
  1666.2 17.9 copy-start.18
  1682.4 203.7 %copy-start.10 = (f32[12,8]{1,0:T(8,128)}, f32[12,8]{1,0:T(8,128)S(1)}, u32[]{:S(2)}) copy-start(f32[12,8]{1,0:T(8,128)S(1)} %get-tuple-element.344) | copy-start | bytes 1156
  1682.4 203.7 %copy-start.11 = (f32[12,8]{1,0:T(8,128)}, f32[12,8]{1,0:T(8,128)S(1)}, u32[]{:S(2)}) copy-start(f32[12,8]{1,0:T(8,128)S(1)} %get-tuple-element.345) | copy-start | bytes 1156
  1682.4 203.7 %copy-start.12 = (f32[12,8]{1,0:T(8,128)}, f32[12,8]{1,0:T(8,128)S(1)}, u32[]{:S(2)}) copy-start(f32[12,8]{1,0:T(8,128)S(1)} %get-tuple-element.346) | copy-start | bytes 1156
  1713.4 164.5 %copy-start.19 = (f32[12,16]{1,0:T(8,128)S(1)}, f32[12,16]{1,0:T(8,128)}, u32[]{:S(2)}) copy-start(f32[12,16]{1,0:T(8,128)} %copy-done.18) | copy-start | bytes 2308
  1782.9 103.6 %copy-start.33 = (f32[1,8]{1,0:T(1,128)S(1)}, f32[1,8]{1,0:T(1,128)}, u32[]{:S(2)}) copy-start(f32[1,8]{1,0:T(1,128)} %copy-done.32) | copy-start | bytes 100
  1782.9 103.6 %copy-start.35 = (f32[1,8]{1,0:T(1,128)S(1)}, f32[1,8]{1,0:T(1,128)}, u32[]{:S(2)}) copy-start(f32[1,8]{1,0:T(1,128)} %copy-done.34) | copy-start | bytes 100
  1782.9 103.6 %copy-start.37 = (f32[1,8]{1,0:T(1,128)S(1)}, f32[1,8]{1,0:T(1,128)}, u32[]{:S(2)}) copy-start(f32[1,8]{1,0:T(1,128)} %copy-done.36) | copy-start | bytes 100
  1886.4 12.6 copy-start.74
  1886.4 12.8 copy-start.51
  1886.4 12.8 copy-start.53
  1886.4 12.8 copy-start.55
  1886.4 12.8 copy-start.69
  1886.5 12.7 copy-start.67
  1886.5 12.7 copy-start.43
  1886.5 12.7 copy-start.45
  1886.5 12.7 copy-start.47
  1886.6 12.7 copy-start.71
  (47 other events, 164.3 us)
